TPU v7x, 32 devices: a whole 2x2x4 slice. The times are simulated.
32 devices in a mesh: alpha: 2 (over x), beta: 16 (over z, y, core).
Axes of the slice: x: 2, y: 2, z: 4, core: 2. Of those that a mesh axis runs over, the one named last changes fastest.
Arguments:
- coef: bfloat16 [2048, 2048], P('alpha', 'beta'), may hold values from -6 to 6
- beta_ops: bfloat16 [2048, 512], P('beta'), may hold values from -0.25 to 0.25
- beta_cols: int32 [16, 4], P('beta'), may hold values from 0 to 15, as said below
- alpha_ops: bfloat16 [2048, 4096], P('alpha'), may hold values from -0.09375 to 0.09375
- alpha_cols: int32 [2, 4], P('alpha'), may hold values from 0 to 1, as said below
- pair_alpha: bfloat16 [2048, 576], P('alpha'), may hold values from -12 to 12
- pair_beta: bfloat16 [2048, 576], P('beta'), may hold values from -0.125 to 0.125
- pair_coupling: bfloat16 [576, 576], replicated, may hold values from -0.25 to 0.25
- denominators: float32 [2048, 2048], P('alpha', 'beta'), may hold values from 0.5 to 4
Outputs:
- sigma_scaled: float32 [2048, 2048], P('alpha', 'beta')
Inputs may be any that keep to these rules, and one draw needn't show every extreme that they name: `beta_cols`: the 4 entries of row j are different and each lies within two blocks of j, counted around the beta blocks cyclically. `alpha_cols`: each entry of row i is i or one of its two neighbours, counted around the alpha blocks cyclically; entries may repeat.
All inputs are finite; a program needn't handle non-finite values.
Results may differ from a plain program's by a relative error of at most 0.013.
Values may be sent and summed in bfloat16 or wider, within the bound.
A program may use at most 128 MiB of HBM per device.

v0:
```python
import jax
import jax.numpy as jnp
from jax import lax
from jax.sharding import PartitionSpec as P


def padded(block, sides, width):
    for axis, dim in sides:
        count = lax.axis_size(axis)
        forward = [(i, i + 1) for i in range(count - 1)]
        forward.append((count - 1, 0))
        backward = [(target, source) for source, target in forward]
        low = lax.ppermute(
            lax.slice_in_dim(block, block.shape[dim] - width, None, axis=dim), axis, forward
        )
        high = lax.ppermute(lax.slice_in_dim(block, 0, width, axis=dim), axis, backward)
        block = jnp.concatenate([low, block, high], axis=dim)
    return block


def shifted(block, axis, distance):
    devices = range(lax.axis_size(axis))
    route = [((i - distance) % len(devices), i) for i in devices]
    return lax.ppermute(block, axis, route)


def spread_blocks(operator_blocks, listed_cols, block_width, block_count):
    row_count = operator_blocks.shape[0]
    listed = listed_cols.shape[0]
    onehot = (listed_cols[:, None] == jnp.arange(block_count, dtype=jnp.int32)[None, :]).astype(
        jnp.bfloat16
    )
    tile_set = operator_blocks.reshape(row_count, listed, block_width)
    placed = jnp.einsum("rkc,kn->rnc", tile_set, onehot, preferred_element_type=jnp.float32)
    return placed.astype(jnp.bfloat16).reshape(row_count, block_count * block_width)


def local(
    coef,
    beta_ops,
    beta_cols,
    alpha_ops,
    alpha_cols,
    pair_alpha,
    pair_beta,
    pair_coupling,
    denominators,
):
    alpha_width = coef.shape[0]
    beta_width = coef.shape[1]
    beta_count = lax.axis_size("beta")
    alpha_count = lax.axis_size("alpha")
    beta_slots = (beta_cols[0] - lax.axis_index("beta") + 2 + beta_count) % beta_count
    beta_near_ops = spread_blocks(beta_ops, beta_slots, beta_width, 5)
    middle = padded(coef, (("beta", 1),), beta_width)
    lowest = shifted(coef, "beta", 2)
    highest = shifted(coef, "beta", -2)
    beta_span = jnp.concatenate([lowest, middle, highest], axis=1)
    same_beta = lax.dot_general(
        beta_span, beta_near_ops, (((1,), (1,)), ((), ())), preferred_element_type=jnp.float32
    )
    alpha_slots = (alpha_cols[0] - lax.axis_index("alpha") + 1 + alpha_count) % alpha_count
    alpha_near = spread_blocks(alpha_ops, alpha_slots, alpha_width, 3)
    alpha_span = padded(coef, (("alpha", 0),), alpha_width)
    same_alpha = jnp.dot(alpha_near, alpha_span, preferred_element_type=jnp.float32)
    partial_density = jnp.dot(coef, pair_beta, preferred_element_type=jnp.float32)
    share = lax.psum_scatter(
        partial_density.astype(jnp.bfloat16), "beta", scatter_dimension=0, tiled=True
    )
    share_rows = share.shape[0]
    alpha_rows = lax.dynamic_slice_in_dim(
        pair_alpha, lax.axis_index("beta") * share_rows, share_rows, 0
    )
    local_rows = (
        jnp.dot(share, pair_coupling, preferred_element_type=jnp.float32)
        * alpha_rows.astype(jnp.float32)
    ).astype(jnp.bfloat16)
    excited = lax.all_gather(local_rows, "beta", axis=0, tiled=True)
    mixed = lax.dot_general(
        excited, pair_beta, (((1,), (1,)), ((), ())), preferred_element_type=jnp.float32
    )
    return (same_beta + same_alpha + mixed) / denominators


def solution(mesh):
    return jax.shard_map(
        local,
        mesh=mesh,
        in_specs=(
            P("alpha", "beta"),
            P("beta", None),
            P("beta", None),
            P("alpha", None),
            P("alpha", None),
            P("alpha", None),
            P("beta", None),
            P(),
            P("alpha", "beta"),
        ),
        out_specs=P("alpha", "beta"),
        check_vma=False,
    )
```

profile of v0, /device:TPU:0, one launch (start us, length us, event | category | flops | bytes accessed | tf_op | source)
XLA Modules:
  0.0 124.2 jit_solution(1075541897015316540)
XLA Ops:
  6.5 0.0 copy-start
  6.5 0.0 copy-start.1
  6.5 0.0 reduce-scatter.2.cloned.1.call-start
  6.5 2.8 %convolution_convert_fusion = bf16[1024,576]{1,0:T(8,128)(2,1)} fusion(bf16[1024,128]{1,0:T(8,128)(2,1)} %param.9, bf16[128,576]{0,1:T(8,128)(2,1)} %param.15), kind=kOutput, calls=%fused_computation.1 | convolution fusion | flops 151584768 | bytes 1589248 | tf_op jit(solution)/shard_map/dot_general | solution.py:66
  9.3 0.0 reduce-scatter.2.cloned.1.call-update
  9.3 0.0 all-gather.2.cloned.1.call-start
  9.4 0.0 copy-done.1
  9.4 3.0 %collective-permute-start.5 = (bf16[1024,128]{1,0:T(8,128)(2,1)S(1)}, bf16[1024,128]{1,0:T(8,128)(2,1)}, u32[]{:S(2)}, u32[]{:S(2)}) collective-permute-start(bf16[1024,128]{1,0:T(8,128)(2,1)S(1)} %copy-done.1), channel_id=1, source_target_pairs={{16,0},{0,16},{17,1},{1,17},{18,2},{2,18},{19,3},{3,19},{20,4},{4,... | collective-permute-start | bytes 786440 | tf_op jit(solution)/shard_map/ppermute | solution.py:16
  12.4 0.1 collective-permute-start.4
  12.5 2.0 %collective-permute-start = (bf16[1024,128]{1,0:T(8,128)(2,1)S(1)}, bf16[1024,128]{1,0:T(8,128)(2,1)S(1)}, u32[]{:S(2)}, u32[]{:S(2)}) collective-permute-start(bf16[1024,128]{1,0:T(8,128)(2,1)S(1)} %copy-done.1), channel_id=1, source_target_pairs={{14,0},{15,1},{0,2},{1,3},{2,4},{3,5},{4,6},{5,7},{6,8},{7,9},{8,1... | collective-permute-start | bytes 786440 | tf_op jit(solution)/shard_map/ppermute | solution.py:24
  14.5 0.0 collective-permute-start.1
  14.5 4.4 %collective-permute-start.2 = (bf16[1024,128]{1,0:T(8,128)(2,1)S(1)}, bf16[1024,128]{1,0:T(8,128)(2,1)S(1)}, u32[]{:S(2)}, u32[]{:S(2)}) collective-permute-start(bf16[1024,128]{1,0:T(8,128)(2,1)S(1)} %copy-done.1), channel_id=1, source_target_pairs={{1,0},{2,1},{3,2},{4,3},{5,4},{6,5},{7,6},{8,7},{9,8},{10,9},{11,1... | collective-permute-start | bytes 786440 | tf_op jit(solution)/shard_map/ppermute | solution.py:16
  18.9 0.0 copy-done
  18.9 0.1 constant_dynamic-slice_fusion
  19.0 0.1 copy.15
  19.2 0.0 copy-start.8
  19.2 0.0 copy-start.2
  19.2 14.7 %reshape.56 = bf16[1024,4,1024]{2,1,0:T(4,128)(2,1)} reshape(bf16[1024,4096]{1,0:T(8,128)(2,1)} %param.12) | data formatting | bytes 16777216 | tf_op jit(solution)/shard_map/reshape | solution.py:33
  33.9 0.0 copy-done.8
  33.9 38.3 %reduce-scatter.2.cloned.1.call-done = bf16[64,576]{1,0:T(8,128)(2,1)} async-done(((bf16[1024,576]{1,0:T(8,128)(2,1)}), bf16[64,576]{1,0:T(8,128)(2,1)}) %reduce-scatter.2.cloned.1.call-update) | async-done | bytes 73744 | tf_op jit(solution)/shard_map/reduce_scatter | solution.py:67
  72.3 0.0 copy-done.2
  72.3 1.8 %fusion.3 = bf16[64,576]{1,0:T(8,128)(2,1)} fusion(bf16[64,576]{1,0:T(8,128)(2,1)} %reduce-scatter.2.cloned.1.call-done, bf16[576,576]{1,0:T(8,128)(2,1)S(1)} %copy-done.2, bf16[64,576]{1,0:T(8,128)(2,1)S(1)} %copy.15), kind=kOutput, calls=%fused_computation.8 | convolution fusion | flops 42577920 | bytes 884736 | tf_op jit(solution)/shard_map/dot_general | solution.py:75
  74.0 0.0 all-gather.2.cloned.1.call-update
  74.1 0.0 copy-start.9
  74.1 9.6 %convert_bitcast_fusion = bf16[1024,3,1024]{2,1,0:T(4,128)(2,1)} fusion(bf16[1024,4,1024]{2,1,0:T(4,128)(2,1)} %reshape.56, s32[4]{0:T(128)S(1)} %and_select_fusion), kind=kOutput, calls=%fused_computation | convolution fusion | flops 28311564 | bytes 14680080 | tf_op jit(solution)/shard_map/rkc,kn->rnc/dot_general | solution.py:34
  83.7 0.0 copy-done.9
  83.7 0.0 copy-start.7
  83.7 13.1 %copy.13 = bf16[1024,3,1024]{0,2,1:T(8,128)(2,1)} copy(bf16[1024,3,1024]{2,1,0:T(4,128)(2,1)} %convert_bitcast_fusion) | data formatting | bytes 12582912 | tf_op jit(solution)/shard_map/convert_element_type | solution.py:35
  96.9 0.0 copy-done.7
  96.9 0.3 fusion.2
  97.2 0.2 copy.12
  97.4 0.0 collective-permute-done
  97.5 0.0 copy-start.6
  97.5 0.7 copy-done.6
  98.2 2.4 %collective-permute-start.3 = (bf16[1024,128]{1,0:T(8,128)(2,1)S(1)}, bf16[1024,128]{1,0:T(8,128)(2,1)S(1)}, u32[]{:S(2)}, u32[]{:S(2)}) collective-permute-start(bf16[1024,128]{1,0:T(8,128)(2,1)S(1)} %copy-done.1), channel_id=1, source_target_pairs={{2,0},{3,1},{4,2},{5,3},{6,4},{7,5},{8,6},{9,7},{10,8},{11,9},{12,... | collective-permute-start | bytes 786440 | tf_op jit(solution)/shard_map/ppermute | solution.py:24
  100.5 1.0 constant_dynamic-update-slice_fusion.4
  101.5 0.0 collective-permute-done.1
  101.5 0.1 constant_dynamic-update-slice_fusion.3
  101.6 0.1 constant_dynamic-update-slice_fusion.2
  101.7 0.0 collective-permute-done.2
  101.7 0.1 constant_dynamic-update-slice_fusion.1
  101.8 6.3 %collective-permute-done.3 = bf16[1024,128]{1,0:T(8,128)(2,1)S(1)} collective-permute-done((bf16[1024,128]{1,0:T(8,128)(2,1)S(1)}, bf16[1024,128]{1,0:T(8,128)(2,1)S(1)}, u32[]{:S(2)}, u32[]{:S(2)}) %collective-permute-start.3) | collective-permute-done | bytes 262176 | tf_op jit(solution)/shard_map/ppermute | solution.py:24
  108.0 0.1 constant_dynamic-update-slice_fusion
  108.1 0.0 collective-permute-done.5
  108.1 0.0 collective-permute-done.4
  108.1 0.0 copy-start.3
  108.1 5.5 %fusion.4 = f32[1024,128]{1,0:T(8,128)} fusion(bf16[1024,3072]{0,1:T(8,128)(2,1)} %bitcast.27, bf16[1024,128]{1,0:T(8,128)(2,1)} %collective-permute-done.5, bf16[1024,128]{1,0:T(8,128)(2,1)S(1)} %copy-done.1, bf16[1024,128]{1,0:T(8,128)(2,1)} %collective-permute-done.4), kind=kOutput, calls=%fused_computation.9 | convolution fusion | flops 807665664 | bytes 7602176 | tf_op jit(solution)/shard_map/dot_general | solution.py:65
  113.7 0.5 all-gather.2.cloned.1.call-done
  114.1 0.0 copy-done.3
  114.1 0.0 copy-start.4
  114.1 0.0 copy-start.5
  114.1 1.9 %fusion.19 = f32[1024,128]{1,0:T(8,128)S(1)} fusion(bf16[1024,576]{1,0:T(8,128)(2,1)} %all-gather.2.cloned.1.call-done, bf16[128,576]{0,1:T(8,128)(2,1)S(1)} %copy-done.3), kind=kOutput, calls=%fused_computation.36 | convolution fusion | flops 150994944 | bytes 1851392 | tf_op jit(solution)/shard_map/dot_general | solution.py:79
  116.0 0.0 copy-done.4
  116.0 0.0 copy-done.5
  116.0 1.3 %fusion.1 = f32[1024,128]{1,0:T(8,128)} fusion(f32[1024,128]{1,0:T(8,128)S(1)} %copy-done.4, f32[1024,128]{1,0:T(8,128)S(1)} %fusion.19, f32[1024,128]{1,0:T(8,128)S(1)} %copy-done.5, bf16[1024,640]{1,0:T(8,128)(2,1)S(1)} %constant_dynamic-update-slice_fusion, bf16[128,640]{0,1:T(8,128)(2,1)S(1)} %bitcast.28), kind=kOutput, calls=%fused_computation.4 | convolution fusion | flops 168165376 | bytes 3571712 | tf_op jit(solution)/shard_map/dot_general | solution.py:59
  (3 shorter events, 0.1 us)
Async XLA Ops:
  6.5 12.4 %copy-start = (bf16[1024,576]{0,1:T(8,128)(2,1)S(1)}, bf16[1024,576]{0,1:T(8,128)(2,1)}, u32[]{:S(2)}) copy-start(bf16[1024,576]{0,1:T(8,128)(2,1)} %param.14) | copy-start | bytes 3538948
  6.5 2.8 %copy-start.1 = (bf16[1024,128]{1,0:T(8,128)(2,1)S(1)}, bf16[1024,128]{1,0:T(8,128)(2,1)}, u32[]{:S(2)}) copy-start(bf16[1024,128]{1,0:T(8,128)(2,1)} %param.9) | copy-start | bytes 786436
  6.5 65.7 %reduce-scatter.2.cloned.1.call-start = ((), (), s32[]{:S(2)}) async-start(), calls=%async_computation.1 | async-start | bytes 1392640 | tf_op jit(solution)/shard_map/reduce_scatter | solution.py:67
  9.3 104.8 %all-gather.2.cloned.1.call-start = ((), (), s32[]{:S(2)}) async-start(), calls=%async_computation.2 | async-start | bytes 1392640 | tf_op jit(solution)/shard_map/all_gather | solution.py:78
  9.4 98.7 %collective-permute-start.5 = (bf16[1024,128]{1,0:T(8,128)(2,1)S(1)}, bf16[1024,128]{1,0:T(8,128)(2,1)}, u32[]{:S(2)}, u32[]{:S(2)}) collective-permute-start(bf16[1024,128]{1,0:T(8,128)(2,1)S(1)} %copy-done.1), channel_id=1, source_target_pairs={{16,0},{0,16},{17,1},{1,17},{18,2},{2,18},{19,3},{3,19},{20,4},{4,... | collective-permute-start | bytes 786440 | tf_op jit(solution)/shard_map/ppermute | solution.py:16
  12.4 95.7 %collective-permute-start.4 = (bf16[1024,128]{1,0:T(8,128)(2,1)S(1)}, bf16[1024,128]{1,0:T(8,128)(2,1)}, u32[]{:S(2)}, u32[]{:S(2)}) collective-permute-start(bf16[1024,128]{1,0:T(8,128)(2,1)S(1)} %copy-done.1), channel_id=1, source_target_pairs={{0,16},{16,0},{1,17},{17,1},{2,18},{18,2},{3,19},{19,3},{4,20},{20... | collective-permute-start | bytes 786440 | tf_op jit(solution)/shard_map/ppermute | solution.py:13
  12.5 85.0 %collective-permute-start = (bf16[1024,128]{1,0:T(8,128)(2,1)S(1)}, bf16[1024,128]{1,0:T(8,128)(2,1)S(1)}, u32[]{:S(2)}, u32[]{:S(2)}) collective-permute-start(bf16[1024,128]{1,0:T(8,128)(2,1)S(1)} %copy-done.1), channel_id=1, source_target_pairs={{14,0},{15,1},{0,2},{1,3},{2,4},{3,5},{4,6},{5,7},{6,8},{7,9},{8,1... | collective-permute-start | bytes 786440 | tf_op jit(solution)/shard_map/ppermute | solution.py:24
  14.5 87.1 %collective-permute-start.1 = (bf16[1024,128]{1,0:T(8,128)(2,1)S(1)}, bf16[1024,128]{1,0:T(8,128)(2,1)S(1)}, u32[]{:S(2)}, u32[]{:S(2)}) collective-permute-start(bf16[1024,128]{1,0:T(8,128)(2,1)S(1)} %copy-done.1), channel_id=1, source_target_pairs={{0,1},{1,2},{2,3},{3,4},{4,5},{5,6},{6,7},{7,8},{8,9},{9,10},{10,1... | collective-permute-start | bytes 786440 | tf_op jit(solution)/shard_map/ppermute | solution.py:13
  14.5 87.2 %collective-permute-start.2 = (bf16[1024,128]{1,0:T(8,128)(2,1)S(1)}, bf16[1024,128]{1,0:T(8,128)(2,1)S(1)}, u32[]{:S(2)}, u32[]{:S(2)}) collective-permute-start(bf16[1024,128]{1,0:T(8,128)(2,1)S(1)} %copy-done.1), channel_id=1, source_target_pairs={{1,0},{2,1},{3,2},{4,3},{5,4},{6,5},{7,6},{8,7},{9,8},{10,9},{11,1... | collective-permute-start | bytes 786440 | tf_op jit(solution)/shard_map/ppermute | solution.py:16
  19.2 14.8 %copy-start.8 = (s32[1,4]{1,0:T(1,128)S(1)}, s32[1,4]{1,0:T(1,128)}, u32[]{:S(2)}) copy-start(s32[1,4]{1,0:T(1,128)} %param.13) | copy-start | bytes 52
  19.2 53.1 %copy-start.2 = (bf16[576,576]{1,0:T(8,128)(2,1)S(1)}, bf16[576,576]{1,0:T(8,128)(2,1)}, u32[]{:S(2)}) copy-start(bf16[576,576]{1,0:T(8,128)(2,1)} %param.16) | copy-start | bytes 1990660
  74.1 9.6 %copy-start.9 = (s32[1,4]{1,0:T(1,128)S(1)}, s32[1,4]{1,0:T(1,128)}, u32[]{:S(2)}) copy-start(s32[1,4]{1,0:T(1,128)} %param.11) | copy-start | bytes 52
  83.7 13.2 %copy-start.7 = (bf16[128,512]{1,0:T(8,128)(2,1)S(1)}, bf16[128,512]{1,0:T(8,128)(2,1)}, u32[]{:S(2)}) copy-start(bf16[128,512]{1,0:T(8,128)(2,1)} %param.10) | copy-start | bytes 393220
  97.5 0.7 copy-start.6
  98.2 9.9 %collective-permute-start.3 = (bf16[1024,128]{1,0:T(8,128)(2,1)S(1)}, bf16[1024,128]{1,0:T(8,128)(2,1)S(1)}, u32[]{:S(2)}, u32[]{:S(2)}) collective-permute-start(bf16[1024,128]{1,0:T(8,128)(2,1)S(1)} %copy-done.1), channel_id=1, source_target_pairs={{2,0},{3,1},{4,2},{5,3},{6,4},{7,5},{8,6},{9,7},{10,8},{11,9},{12,... | collective-permute-start | bytes 786440 | tf_op jit(solution)/shard_map/ppermute | solution.py:24
  108.1 6.0 %copy-start.3 = (bf16[128,576]{0,1:T(8,128)(2,1)S(1)}, bf16[128,576]{0,1:T(8,128)(2,1)}, u32[]{:S(2)}) copy-start(bf16[128,576]{0,1:T(8,128)(2,1)} %param.15) | copy-start | bytes 442372
  114.1 1.9 %copy-start.4 = (f32[1024,128]{1,0:T(8,128)S(1)}, f32[1024,128]{1,0:T(8,128)}, u32[]{:S(2)}) copy-start(f32[1024,128]{1,0:T(8,128)} %param.17) | copy-start | bytes 1572868
  114.1 1.9 %copy-start.5 = (f32[1024,128]{1,0:T(8,128)S(1)}, f32[1024,128]{1,0:T(8,128)}, u32[]{:S(2)}) copy-start(f32[1024,128]{1,0:T(8,128)} %fusion.4) | copy-start | bytes 1572868
Sparse Core Ops, SparseCore 0:
  11.0 61.2 reduce-scatter.1
  74.5 39.5 all-gather.1
where the time goes:
time: 125 us; the launch traced here: 124 us
  waiting for transfers between devices  45.1 us (36%)
  local copies, waits for them, and re-layouts  30.4 us (24%)
  matrix products  23.2 us (19%)
  between operations  13.6 us (11%)
  starting transfers between devices  11.9 us (10%)
    reduce_scatter x1, waiting for transfers between devices, local(): lax.psum_scatter(partial_density.astype(jnp.bfloat16), 'beta', scatter_di...  38.3 us
    reshape x2, local copies, waits for them, and re-layouts, spread_blocks(): tile_set = operator_blocks.reshape(row_count, listed, block_width)  14.8 us
    convert_element_type x2, local copies, waits for them, and re-layouts, spread_blocks(): placed.astype(jnp.bfloat16).reshape(row_count, block_count * block_width)  13.4 us
    dot_general x2, matrix products, spread_blocks(): jnp.einsum('rkc,kn->rnc', tile_set, onehot, preferred_element_type=jnp.fl...  9.93 us
    ppermute x2, starting transfers between devices, padded(): lax.ppermute(lax.slice_in_dim(block, 0, width, axis=dim), axis, backward)  7.47 us
    ppermute x2, waiting for transfers between devices, shifted(): return lax.ppermute(block, axis, route)  6.29 us
    dot_general x1, matrix products, local(): jnp.dot(alpha_near, alpha_span, preferred_element_type=jnp.float32)  5.5 us
    ppermute x2, starting transfers between devices, shifted(): return lax.ppermute(block, axis, route)  4.33 us
  transfers between devices with their start and end apart: 8, of which 3 were waited for; matrix products, arithmetic and copies ran while one was open for 38% of the time, Pallas kernels for 0%

commit v1 on v0

v1 whole, which is shorter than its diff:
```python
import functools

import jax
import jax.numpy as jnp
from jax import lax
from jax.experimental import pallas as pl
from jax.experimental.pallas import tpu as pltpu
from jax.sharding import PartitionSpec as P

MESH = pl.DeviceIdType.MESH
GROUP = 4
REACH = 2
F32 = jnp.float32
BF16 = jnp.bfloat16


def kernel(
    n_alpha,
    n_beta,
    beta_cols,
    alpha_cols,
    coef_in,
    ops_in,
    alpha_in,
    pair_alpha_in,
    pair_beta_in,
    coupling_in,
    out,
    coef,
    ops,
    alpha_ops,
    pair_alpha,
    pair_beta,
    coupling,
    near,
    window,
    part,
    part_in,
    excited,
    both,
    back,
    back_in,
    local_sem,
    alpha_sem,
    coef_send,
    coef_recv,
    pair_send,
    pair_recv,
    near_send,
    near_recv,
    back_send,
    back_recv,
    part_send,
    part_recv,
    exc_send,
    exc_recv,
    halo_send,
    halo_recv,
    nbr_send,
    nbr_recv,
):
    a = lax.axis_index("alpha")
    b = lax.axis_index("beta")
    outer = n_beta // GROUP
    g = b % GROUP
    z = b // GROUP
    rows, width = coef.shape[1], coef.shape[2]
    strip = rows // GROUP
    share = strip // outer
    listed = beta_cols.shape[1]
    alpha_listed = alpha_cols.shape[1]
    pairs = coupling.shape[0]

    def local(index, src, dst, sem=None):
        copy = pltpu.make_async_copy(src, dst, local_sem.at[index] if sem is None else sem)
        copy.start()
        return copy

    def remote(src, dst, send, recv, target):
        copy = pltpu.make_async_remote_copy(
            src_ref=src,
            dst_ref=dst,
            send_sem=send,
            recv_sem=recv,
            device_id=target,
            device_id_type=MESH,
        )
        copy.start()
        return copy

    def mate(d):
        return (a, z * GROUP + (g + d) % GROUP)

    def plane(d):
        return (a, ((z + d) % outer) * GROUP + g)

    alpha_steps = [1] if n_alpha > 1 else []
    if n_alpha > 2:
        alpha_steps.append(n_alpha - 1)

    own_coef = local(0, coef_in, coef.at[0])
    own_pair = local(1, pair_beta_in, pair_beta.at[g])
    own_strip = local(
        2, coef_in.at[pl.ds(pl.multiple_of(g * strip, strip), strip)], window.at[REACH + g]
    )
    own_ops = local(3, ops_in, ops)
    own_coupling = local(4, coupling_in, coupling)
    first = pl.multiple_of(g * strip + z * share, share)
    own_rows = local(5, pair_alpha_in.at[pl.ds(first, share)], pair_alpha)
    alpha_copy = local(0, alpha_in, alpha_ops, alpha_sem)

    barrier = pltpu.get_barrier_semaphore()
    partners = 0
    for d in range(1, GROUP):
        pl.semaphore_signal(barrier, inc=1, device_id=mate(d), device_id_type=MESH)
        partners += 1
    for d in range(1, outer):
        pl.semaphore_signal(barrier, inc=1, device_id=plane(d), device_id_type=MESH)
        partners += 1
    for d in alpha_steps:
        pl.semaphore_signal(
            barrier, inc=1, device_id=((a + d) % n_alpha, b), device_id_type=MESH
        )
        partners += 1
    pl.semaphore_wait(barrier, partners)

    own_coef.wait()
    coef_copies = []
    for d in (2, 3, 1):
        h = (g + d) % GROUP
        coef_copies.append(
            remote(
                coef.at[0, pl.ds(pl.multiple_of(h * strip, strip), strip)],
                window.at[REACH + g],
                coef_send.at[d],
                coef_recv.at[d],
                mate(d),
            )
        )
    own_pair.wait()
    pair_copies = [
        remote(
            pair_beta.at[g], pair_beta.at[g], pair_send.at[d], pair_recv.at[d], mate(d)
        )
        for d in (2, 3, 1)
    ]
    alpha_copies = [
        remote(
            coef.at[0],
            coef.at[2 - i if n_alpha > 2 else 1],
            nbr_send.at[i],
            nbr_recv.at[i],
            ((a + d) % n_alpha, b),
        )
        for i, d in enumerate(alpha_steps)
    ]

    own_ops.wait()
    tiles = [ops[:, k * width : (k + 1) * width] for k in range(listed)]
    slots = [(beta_cols[0, k] - b + REACH + n_beta) % n_beta for k in range(listed)]
    for s in range(2 * REACH + 1):
        total = jnp.zeros(tiles[0].shape, F32)
        for k in range(listed):
            chosen = (slots[k] == s).astype(F32)
            total = total + tiles[k].astype(F32) * chosen
        near[g, :, s * width : (s + 1) * width] = total.astype(BF16)
    near_copies = [
        remote(near.at[g], near.at[g], near_send.at[d], near_recv.at[d], mate(d))
        for d in (2, 3, 1)
    ]

    own_strip.wait()
    for copy in coef_copies:
        copy.wait_recv()
    halo_copies = [
        remote(
            window.at[pl.ds(GROUP, REACH)],
            window.at[pl.ds(0, REACH)],
            halo_send.at[0],
            halo_recv.at[0],
            plane(1),
        ),
        remote(
            window.at[pl.ds(REACH, REACH)],
            window.at[pl.ds(REACH + GROUP, REACH)],
            halo_send.at[1],
            halo_recv.at[1],
            plane(outer - 1),
        ),
    ]
    for copy in pair_copies:
        copy.wait_recv()

    strips = jnp.concatenate([window[REACH + i] for i in range(GROUP)], axis=1)
    plane_pairs = pair_beta[...].reshape(GROUP * width, pairs)
    density = jnp.dot(strips, plane_pairs, preferred_element_type=F32)
    part[...] = density.astype(BF16).reshape(outer, share, pairs)
    part_copies = [
        remote(
            part.at[(z + d) % outer],
            part_in.at[d - 1],
            part_send.at[d - 1],
            part_recv.at[d - 1],
            plane(d),
        )
        for d in range(1, outer)
    ]

    for copy in alpha_copies:
        copy.wait_recv()
    alpha_copy.wait()
    blocks = []
    for k in range(alpha_listed):
        off = (alpha_cols[0, k] - a + n_alpha) % n_alpha
        blocks.append(jnp.minimum(off, 1) + jnp.where(off > 1, 1, 0) if n_alpha > 2 else off)

    def alpha_step(i, carry):
        at = pl.ds(pl.multiple_of(i * strip, strip), strip)
        total = jnp.zeros((strip, width), F32)
        for k in range(alpha_listed):
            total = total + jnp.dot(
                alpha_ops[at, k * rows : (k + 1) * rows],
                coef[blocks[k]],
                preferred_element_type=F32,
            )
        out[at, :] = total
        return carry

    lax.fori_loop(0, GROUP, alpha_step, 0)

    for copy in part_copies:
        copy.wait_recv()
    total = part[z].astype(F32)
    for d in range(1, outer):
        total = total + part_in[d - 1].astype(F32)
    own_coupling.wait()
    own_rows.wait()
    raised = jnp.dot(total.astype(BF16), coupling[...], preferred_element_type=F32)
    excited[z] = (raised * pair_alpha[...].astype(F32)).astype(BF16)
    exc_copies = [
        remote(
            excited.at[z], excited.at[z], exc_send.at[d - 1], exc_recv.at[d - 1], plane(d)
        )
        for d in range(1, outer)
    ]

    for copy in near_copies:
        copy.wait_recv()
    for copy in halo_copies:
        copy.wait_recv()
    for i in range(GROUP):
        around = jnp.concatenate([window[i + s] for s in range(2 * REACH + 1)], axis=1)
        both[i] = lax.dot_general(
            around, near[i], (((1,), (1,)), ((), ())), preferred_element_type=F32
        )

    for copy in exc_copies:
        copy.wait_recv()
    rows_excited = excited[...].reshape(strip, pairs)
    back_copies = []
    for d in (2, 3, 1, 0):
        h = (g + d) % GROUP
        mixed = lax.dot_general(
            rows_excited, pair_beta[h], (((1,), (1,)), ((), ())), preferred_element_type=F32
        )
        if d == 0:
            at = pl.ds(pl.multiple_of(g * strip, strip), strip)
            out[at, :] = out[at, :] + (mixed + both[h])
        else:
            back[d - 1] = (mixed + both[h]).astype(BF16)
            back_copies.append(
                (
                    d,
                    remote(
                        back.at[d - 1],
                        back_in.at[d - 1],
                        back_send.at[d - 1],
                        back_recv.at[d - 1],
                        mate(d),
                    ),
                )
            )
    for d, copy in sorted(back_copies, key=lambda pair: pair[0]):
        copy.wait_recv()
        h = (g + GROUP - d) % GROUP
        at = pl.ds(pl.multiple_of(h * strip, strip), strip)
        out[at, :] = out[at, :] + back_in[d - 1].astype(F32)

    everything = coef_copies + pair_copies + alpha_copies + near_copies + halo_copies
    everything += part_copies + exc_copies + [copy for _, copy in back_copies]
    for copy in everything:
        copy.wait_send()


def local(
    coef,
    beta_ops,
    beta_cols,
    alpha_ops,
    alpha_cols,
    pair_alpha,
    pair_beta,
    pair_coupling,
    denominators,
):
    n_alpha = lax.axis_size("alpha")
    n_beta = lax.axis_size("beta")
    rows, width = coef.shape
    pairs = pair_beta.shape[1]
    outer = n_beta // GROUP
    strip = rows // GROUP
    share = strip // outer
    span = 2 * REACH + 1
    dma = pltpu.SemaphoreType.DMA
    vmem, smem, anywhere = (
        pl.BlockSpec(memory_space=pltpu.VMEM),
        pl.BlockSpec(memory_space=pltpu.SMEM),
        pl.BlockSpec(memory_space=pl.ANY),
    )
    summed = pl.pallas_call(
        functools.partial(kernel, n_alpha, n_beta),
        out_shape=jax.ShapeDtypeStruct((rows, width), F32),
        in_specs=[smem, smem] + [anywhere] * 6,
        out_specs=vmem,
        scratch_shapes=[
            pltpu.VMEM((min(n_alpha, 3), rows, width), BF16),
            pltpu.VMEM(beta_ops.shape, BF16),
            pltpu.VMEM(alpha_ops.shape, BF16),
            pltpu.VMEM((share, pairs), BF16),
            pltpu.VMEM((GROUP, width, pairs), BF16),
            pltpu.VMEM((pairs, pairs), BF16),
            pltpu.VMEM((GROUP, width, span * width), BF16),
            pltpu.VMEM((GROUP + 2 * REACH, strip, width), BF16),
            pltpu.VMEM((outer, share, pairs), BF16),
            pltpu.VMEM((outer - 1, share, pairs), BF16),
            pltpu.VMEM((outer, share, pairs), BF16),
            pltpu.VMEM((GROUP, strip, width), F32),
            pltpu.VMEM((GROUP - 1, strip, width), BF16),
            pltpu.VMEM((GROUP - 1, strip, width), BF16),
            dma((6,)),
            dma,
            dma((GROUP,)),
            dma((GROUP,)),
            dma((GROUP,)),
            dma((GROUP,)),
            dma((GROUP,)),
            dma((GROUP,)),
            dma((GROUP - 1,)),
            dma((GROUP - 1,)),
            dma((outer - 1,)),
            dma((outer - 1,)),
            dma((outer - 1,)),
            dma((outer - 1,)),
            dma((2,)),
            dma((2,)),
            dma((2,)),
            dma((2,)),
        ],
        compiler_params=pltpu.CompilerParams(collective_id=0, has_side_effects=True),
    )(beta_cols, alpha_cols, coef, beta_ops, alpha_ops, pair_alpha, pair_beta, pair_coupling)
    return summed / denominators


def solution(mesh):
    return jax.shard_map(
        local,
        mesh=mesh,
        in_specs=(
            P("alpha", "beta"),
            P("beta", None),
            P("beta", None),
            P("alpha", None),
            P("alpha", None),
            P("alpha", None),
            P("beta", None),
            P(),
            P("alpha", "beta"),
        ),
        out_specs=P("alpha", "beta"),
        check_vma=False,
    )
```

time: 125 us -> 44.6 us (0.36)
  waiting for transfers between devices: 45.1 us -> 0 us
  Pallas kernels: 0 us -> 38.3 us
  local copies, waits for them, and re-layouts: 30.4 us -> 4.13 us
  matrix products: 23.2 us -> 0 us
  between operations: 13.6 us -> 0.02 us
  starting transfers between devices: 11.9 us -> 0 us
  other arithmetic: 0.02 us -> 1.91 us
    reduce_scatter x1 -> x0, waiting for transfers between devices: 38.3 us -> none  [local(): lax.psum_scatter(partial_density.astype(jnp.bfloat16), 'beta', scatter_di...]
    pallas_call x0 -> x1, Pallas kernels: none -> 38.3 us  [local(): pl.pallas_call(functools.partial(kernel, n_alpha, n_beta), out_shape=jax....]
    dot_general x7 -> x0, matrix products: 23.2 us -> none  [the longest x2 9.93 us: spread_blocks(): jnp.einsum('rkc,kn->rnc', tile_set, onehot, preferred_element_type=jnp.fl...]
    reshape x2 -> x0, local copies, waits for them, and re-layouts: 14.8 us -> none  [spread_blocks(): tile_set = operator_blocks.reshape(row_count, listed, block_width)]
    convert_element_type x2 -> x0, local copies, waits for them, and re-layouts: 13.4 us -> none  [spread_blocks(): placed.astype(jnp.bfloat16).reshape(row_count, block_count * block_width)]
    ppermute x6 -> x0, starting transfers between devices: 11.9 us -> none  [the longest x2 7.47 us: padded(): lax.ppermute(lax.slice_in_dim(block, 0, width, axis=dim), axis, backward)]
    ppermute x6 -> x0, waiting for transfers between devices: 6.3 us -> none  [the longest x2 6.29 us: shifted(): return lax.ppermute(block, axis, route)]
    unnamed x25 -> x4, local copies, waits for them, and re-layouts: 2.07 us -> 4.13 us
  transfers between devices with their start and end apart: 8 -> 0, of which waited for: 3 -> 0; matrix products, arithmetic and copies ran while one was open for 38% -> 0% of each run, Pallas kernels for 0% -> 0%
where the time goes in v1:
time: 44.6 us; the launch traced here: 44.3 us
  Pallas kernels  38.3 us (86%)
  local copies, waits for them, and re-layouts  4.13 us (9%)
  other arithmetic  1.91 us (4%)
    pallas_call x1, Pallas kernels, local(): pl.pallas_call(functools.partial(kernel, n_alpha, n_beta), out_shape=jax....  38.3 us
    unnamed x4, local copies, waits for them, and re-layouts  4.13 us
    div x1, other arithmetic, local(): return summed / denominators  1.91 us

profile of v1, /device:TPU:0, one launch (start us, length us, event | category | flops | bytes accessed | tf_op | source)
XLA Modules:
  0.0 44.3 jit_solution(12567969767575481003)
XLA Ops:
  0.0 1.7 %copy.11.pair_beta_in = bf16[128,576]{1,0:T(8,128)(2,1)} copy(bf16[128,576]{0,1:T(8,128)(2,1)} %param.15) | data formatting | bytes 294912 | tf_op args[6]
  1.7 2.4 %copy.10.pair_alpha_in = bf16[1024,576]{1,0:T(8,128)(2,1)} copy(bf16[1024,576]{0,1:T(8,128)(2,1)} %param.14) | data formatting | bytes 2359296 | tf_op args[5]
  4.1 0.0 copy-start
  4.1 38.3 %shard_map.91 = f32[1024,128]{1,0:T(8,128)} custom-call(s32[1,4]{1,0:T(1,128)} %beta_cols.1, s32[1,4]{1,0:T(1,128)} %alpha_cols.1, bf16[1024,128]{1,0:T(8,128)(2,1)} %coef_in.1, bf16[128,512]{1,0:T(8,128)(2,1)} %ops_in.1, bf16[1024,4096]{1,0:T(8,128)(2,1)} %alpha_in.1, bf16[1024,576]{1,0:T(8,128)(2,1)} %copy.10.pair_alpha_in, ...), custom_call_target="tpu_custom_call" | custom-call | tf_op jit(solution)/shard_map/pallas_call | solution.py:320
  42.4 0.0 copy-done
  42.4 1.9 %div.3 = f32[1024,128]{1,0:T(8,128)} divide(f32[1024,128]{1,0:T(8,128)} %shard_map.91, f32[1024,128]{1,0:T(8,128)S(1)} %copy-done) | non-fusion elementwise | flops 131072 | bytes 1572864 | tf_op jit(solution)/shard_map/div | solution.py:361
Async XLA Ops:
  4.1 38.3 %copy-start = (f32[1024,128]{1,0:T(8,128)S(1)}, f32[1024,128]{1,0:T(8,128)}, u32[]{:S(2)}) copy-start(f32[1024,128]{1,0:T(8,128)} %param.17) | copy-start | bytes 1572868

commit v2 on v1

--- a/solution.py
+++ b/solution.py
@@ -29,6 +29,7 @@
     coef,
     ops,
     alpha_ops,
+    pair_tile,
     pair_alpha,
     pair_beta,
     coupling,
@@ -91,6 +92,10 @@
     def mate(d):
         return (a, z * GROUP + (g + d) % GROUP)
 
+    core_mate = (a, z * GROUP + (g // 2) * 2 + 1 - g % 2)
+    across = (1 - g // 2) * 2 + g % 2
+    chip_mate = (a, z * GROUP + across)
+
     def plane(d):
         return (a, ((z + d) % outer) * GROUP + g)
 
@@ -106,7 +111,10 @@
     own_ops = local(3, ops_in, ops)
     own_coupling = local(4, coupling_in, coupling)
     first = pl.multiple_of(g * strip + z * share, share)
-    own_rows = local(5, pair_alpha_in.at[pl.ds(first, share)], pair_alpha)
+    lanes = pair_tile.shape[1]
+    own_rows = local(
+        5, pair_alpha_in.at[:, pl.ds(pl.multiple_of(first // lanes * lanes, lanes), lanes)], pair_tile
+    )
     alpha_copy = local(0, alpha_in, alpha_ops, alpha_sem)
 
     barrier = pltpu.get_barrier_semaphore()
@@ -139,10 +147,8 @@
         )
     own_pair.wait()
     pair_copies = [
-        remote(
-            pair_beta.at[g], pair_beta.at[g], pair_send.at[d], pair_recv.at[d], mate(d)
-        )
-        for d in (2, 3, 1)
+        remote(pair_beta.at[g], pair_beta.at[g], pair_send.at[i], pair_recv.at[i], target)
+        for i, target in enumerate((chip_mate, core_mate))
     ]
     alpha_copies = [
         remote(
@@ -165,8 +171,8 @@
             total = total + tiles[k].astype(F32) * chosen
         near[g, :, s * width : (s + 1) * width] = total.astype(BF16)
     near_copies = [
-        remote(near.at[g], near.at[g], near_send.at[d], near_recv.at[d], mate(d))
-        for d in (2, 3, 1)
+        remote(near.at[g], near.at[g], near_send.at[i], near_recv.at[i], target)
+        for i, target in enumerate((chip_mate, core_mate))
     ]
 
     own_strip.wait()
@@ -188,12 +194,24 @@
             plane(outer - 1),
         ),
     ]
-    for copy in pair_copies:
+    pair_copies[0].wait_recv()
+    pair_copies.append(
+        remote(
+            pair_beta.at[across],
+            pair_beta.at[across],
+            pair_send.at[2],
+            pair_recv.at[2],
+            core_mate,
+        )
+    )
+    for copy in pair_copies[1:]:
         copy.wait_recv()
 
     strips = jnp.concatenate([window[REACH + i] for i in range(GROUP)], axis=1)
-    plane_pairs = pair_beta[...].reshape(GROUP * width, pairs)
-    density = jnp.dot(strips, plane_pairs, preferred_element_type=F32)
+    plane_pairs = jnp.concatenate([pair_beta[i] for i in range(GROUP)], axis=1)
+    density = lax.dot_general(
+        strips, plane_pairs, (((1,), (1,)), ((), ())), preferred_element_type=F32
+    )
     part[...] = density.astype(BF16).reshape(outer, share, pairs)
     part_copies = [
         remote(
@@ -228,15 +246,25 @@
 
     lax.fori_loop(0, GROUP, alpha_step, 0)
 
+    near_copies[0].wait_recv()
+    near_copies.append(
+        remote(
+            near.at[across], near.at[across], near_send.at[2], near_recv.at[2], core_mate
+        )
+    )
+    own_rows.wait()
+    pair_alpha[...] = jnp.transpose(pair_tile[...].astype(F32))
+    own_coupling.wait()
+
     for copy in part_copies:
         copy.wait_recv()
     total = part[z].astype(F32)
     for d in range(1, outer):
         total = total + part_in[d - 1].astype(F32)
-    own_coupling.wait()
-    own_rows.wait()
     raised = jnp.dot(total.astype(BF16), coupling[...], preferred_element_type=F32)
-    excited[z] = (raised * pair_alpha[...].astype(F32)).astype(BF16)
+    excited[z] = (raised * pair_alpha[pl.ds(pl.multiple_of(first % lanes, share), share), :]).astype(
+        BF16
+    )
     exc_copies = [
         remote(
             excited.at[z], excited.at[z], exc_send.at[d - 1], exc_recv.at[d - 1], plane(d)
@@ -244,50 +272,49 @@
         for d in range(1, outer)
     ]
 
-    for copy in near_copies:
+    for copy in near_copies[1:]:
         copy.wait_recv()
     for copy in halo_copies:
         copy.wait_recv()
     for i in range(GROUP):
         around = jnp.concatenate([window[i + s] for s in range(2 * REACH + 1)], axis=1)
-        both[i] = lax.dot_general(
+        both[:, i * width : (i + 1) * width] = lax.dot_general(
             around, near[i], (((1,), (1,)), ((), ())), preferred_element_type=F32
         )
 
-    for copy in exc_copies:
-        copy.wait_recv()
-    rows_excited = excited[...].reshape(strip, pairs)
     back_copies = []
-    for d in (2, 3, 1, 0):
-        h = (g + d) % GROUP
-        mixed = lax.dot_general(
-            rows_excited, pair_beta[h], (((1,), (1,)), ((), ())), preferred_element_type=F32
-        )
-        if d == 0:
-            at = pl.ds(pl.multiple_of(g * strip, strip), strip)
-            out[at, :] = out[at, :] + (mixed + both[h])
-        else:
-            back[d - 1] = (mixed + both[h]).astype(BF16)
+    for e in range(outer):
+        if e > 0:
+            exc_copies[e - 1].wait_recv()
+        y = (z + outer - e) % outer
+        mixed = jnp.dot(excited[y], plane_pairs, preferred_element_type=F32)
+        mixed = mixed + both[pl.ds(pl.multiple_of(y * share, share), share), :]
+        for i in range(GROUP):
+            back[i, y] = mixed[:, i * width : (i + 1) * width].astype(BF16)
+        for d in range(1, GROUP):
             back_copies.append(
                 (
                     d,
+                    y,
                     remote(
-                        back.at[d - 1],
-                        back_in.at[d - 1],
-                        back_send.at[d - 1],
-                        back_recv.at[d - 1],
+                        back.at[(g + d) % GROUP, y],
+                        back_in.at[d - 1, y],
+                        back_send.at[e, d],
+                        back_recv.at[e, d],
                         mate(d),
                     ),
                 )
             )
-    for d, copy in sorted(back_copies, key=lambda pair: pair[0]):
+        at = pl.ds(pl.multiple_of(g * strip + y * share, share), share)
+        out[at, :] = out[at, :] + back[g, y].astype(F32)
+    for d, y, copy in back_copies:
         copy.wait_recv()
         h = (g + GROUP - d) % GROUP
-        at = pl.ds(pl.multiple_of(h * strip, strip), strip)
-        out[at, :] = out[at, :] + back_in[d - 1].astype(F32)
+        at = pl.ds(pl.multiple_of(h * strip + y * share, share), share)
+        out[at, :] = out[at, :] + back_in[d - 1, y].astype(F32)
 
     everything = coef_copies + pair_copies + alpha_copies + near_copies + halo_copies
-    everything += part_copies + exc_copies + [copy for _, copy in back_copies]
+    everything += part_copies + exc_copies + [copy for _, _, copy in back_copies]
     for copy in everything:
         copy.wait_send()
 
@@ -310,6 +337,7 @@
     outer = n_beta // GROUP
     strip = rows // GROUP
     share = strip // outer
+    lanes = max(width, share)
     span = 2 * REACH + 1
     dma = pltpu.SemaphoreType.DMA
     vmem, smem, anywhere = (
@@ -319,24 +347,25 @@
     )
     summed = pl.pallas_call(
         functools.partial(kernel, n_alpha, n_beta),
-        out_shape=jax.ShapeDtypeStruct((rows, width), F32),
+        out_shape=pltpu.VMEM((rows, width), F32),
         in_specs=[smem, smem] + [anywhere] * 6,
         out_specs=vmem,
         scratch_shapes=[
             pltpu.VMEM((min(n_alpha, 3), rows, width), BF16),
             pltpu.VMEM(beta_ops.shape, BF16),
             pltpu.VMEM(alpha_ops.shape, BF16),
-            pltpu.VMEM((share, pairs), BF16),
-            pltpu.VMEM((GROUP, width, pairs), BF16),
+            pltpu.VMEM((pairs, lanes), BF16),
+            pltpu.VMEM((lanes, pairs), F32),
+            pltpu.VMEM((GROUP, pairs, width), BF16),
             pltpu.VMEM((pairs, pairs), BF16),
             pltpu.VMEM((GROUP, width, span * width), BF16),
             pltpu.VMEM((GROUP + 2 * REACH, strip, width), BF16),
             pltpu.VMEM((outer, share, pairs), BF16),
             pltpu.VMEM((outer - 1, share, pairs), BF16),
             pltpu.VMEM((outer, share, pairs), BF16),
-            pltpu.VMEM((GROUP, strip, width), F32),
-            pltpu.VMEM((GROUP - 1, strip, width), BF16),
-            pltpu.VMEM((GROUP - 1, strip, width), BF16),
+            pltpu.VMEM((strip, GROUP * width), F32),
+            pltpu.VMEM((GROUP, outer, share, width), BF16),
+            pltpu.VMEM((GROUP - 1, outer, share, width), BF16),
             dma((6,)),
             dma,
             dma((GROUP,)),
@@ -345,8 +374,8 @@
             dma((GROUP,)),
             dma((GROUP,)),
             dma((GROUP,)),
-            dma((GROUP - 1,)),
-            dma((GROUP - 1,)),
+            dma((outer, GROUP)),
+            dma((outer, GROUP)),
             dma((outer - 1,)),
             dma((outer - 1,)),
             dma((outer - 1,)),
@@ -357,7 +386,7 @@
             dma((2,)),
         ],
         compiler_params=pltpu.CompilerParams(collective_id=0, has_side_effects=True),
-    )(beta_cols, alpha_cols, coef, beta_ops, alpha_ops, pair_alpha, pair_beta, pair_coupling)
+    )(beta_cols, alpha_cols, coef, beta_ops, alpha_ops, pair_alpha.T, pair_beta.T, pair_coupling)
     return summed / denominators
 
 

time: 44.6 us -> 37.1 us (0.83)
  local copies, waits for them, and re-layouts: 4.13 us -> 0.01 us
  Pallas kernels: 38.3 us -> 36 us
  other arithmetic: 1.91 us -> 0.87 us
    unnamed x4 -> x2, local copies, waits for them, and re-layouts: 4.13 us -> 0.01 us
    pallas_call x1, Pallas kernels: 38.3 us -> 36 us  [local(): pl.pallas_call(functools.partial(kernel, n_alpha, n_beta), out_shape=pltp...]
    div x1, other arithmetic: 1.91 us -> 0.87 us  [local(): return summed / denominators]
where the time goes in v2:
time: 37.1 us; the launch traced here: 36.9 us
  Pallas kernels  36 us (97%)
  other arithmetic  0.87 us (2%)
    pallas_call x1, Pallas kernels, local(): pl.pallas_call(functools.partial(kernel, n_alpha, n_beta), out_shape=pltp...  36 us
    div x1, other arithmetic, local(): return summed / denominators  0.87 us

profile of v2, /device:TPU:0, one launch (start us, length us, event | category | flops | bytes accessed | tf_op | source)
XLA Modules:
  0.0 36.9 jit_solution(7380770942372294002)
XLA Ops:
  0.0 0.0 copy-start
  0.0 36.0 %shard_map.91 = f32[1024,128]{1,0:T(8,128)S(1)} custom-call(s32[1,4]{1,0:T(1,128)} %beta_cols.1, s32[1,4]{1,0:T(1,128)} %alpha_cols.1, bf16[1024,128]{1,0:T(8,128)(2,1)} %coef_in.1, bf16[128,512]{1,0:T(8,128)(2,1)} %ops_in.1, bf16[1024,4096]{1,0:T(8,128)(2,1)} %alpha_in.1, bf16[576,1024]{1,0:T(8,128)(2,1)} %bitcast.2, bf16[576,128]{1,0:T(8,128)(2,1)} %bitcast.3, ...), custom_call_target="tpu_custom_call" | custom-call | tf_op jit(solution)/shard_map/pallas_call | solution.py:348
  36.0 0.0 copy-done
  36.0 0.9 %div.3 = f32[1024,128]{1,0:T(8,128)} divide(f32[1024,128]{1,0:T(8,128)S(1)} %shard_map.91, f32[1024,128]{1,0:T(8,128)S(1)} %copy-done) | non-fusion elementwise | flops 131072 | bytes 1572864 | tf_op jit(solution)/shard_map/div | solution.py:390
Async XLA Ops:
  0.0 36.0 %copy-start = (f32[1024,128]{1,0:T(8,128)S(1)}, f32[1024,128]{1,0:T(8,128)}, u32[]{:S(2)}) copy-start(f32[1024,128]{1,0:T(8,128)} %param.17) | copy-start | bytes 1572868

commit v3 on v2

--- a/solution.py
+++ b/solution.py
@@ -9,6 +9,7 @@
 
 MESH = pl.DeviceIdType.MESH
 GROUP = 4
+PIECES = 2
 REACH = 2
 F32 = jnp.float32
 BF16 = jnp.bfloat16
@@ -68,6 +69,7 @@
     rows, width = coef.shape[1], coef.shape[2]
     strip = rows // GROUP
     share = strip // outer
+    sub = share // PIECES
     listed = beta_cols.shape[1]
     alpha_listed = alpha_cols.shape[1]
     pairs = coupling.shape[0]
@@ -99,6 +101,7 @@
     def plane(d):
         return (a, ((z + d) % outer) * GROUP + g)
 
+    far_first = sorted(range(1, outer), key=lambda d: -min(d, outer - d))
     alpha_steps = [1] if n_alpha > 1 else []
     if n_alpha > 2:
         alpha_steps.append(n_alpha - 1)
@@ -133,18 +136,18 @@
     pl.semaphore_wait(barrier, partners)
 
     own_coef.wait()
-    coef_copies = []
-    for d in (2, 3, 1):
-        h = (g + d) % GROUP
-        coef_copies.append(
-            remote(
-                coef.at[0, pl.ds(pl.multiple_of(h * strip, strip), strip)],
-                window.at[REACH + g],
-                coef_send.at[d],
-                coef_recv.at[d],
-                mate(d),
-            )
-        )
+    beside = (g // 2) * 2 + 1 - g % 2
+    opposite = (1 - g // 2) * 2 + 1 - g % 2
+    coef_copies = [
+        remote(
+            coef.at[0, pl.ds(pl.multiple_of(h * strip, strip), strip)],
+            window.at[REACH + g],
+            coef_send.at[i],
+            coef_recv.at[i],
+            (a, z * GROUP + h),
+        )
+        for i, h in enumerate((beside, across, opposite))
+    ]
     own_pair.wait()
     pair_copies = [
         remote(pair_beta.at[g], pair_beta.at[g], pair_send.at[i], pair_recv.at[i], target)
@@ -175,25 +178,23 @@
         for i, target in enumerate((chip_mate, core_mate))
     ]
 
+    half = g // 2
     own_strip.wait()
-    for copy in coef_copies:
-        copy.wait_recv()
-    halo_copies = [
-        remote(
-            window.at[pl.ds(GROUP, REACH)],
-            window.at[pl.ds(0, REACH)],
-            halo_send.at[0],
-            halo_recv.at[0],
-            plane(1),
-        ),
-        remote(
-            window.at[pl.ds(REACH, REACH)],
-            window.at[pl.ds(REACH + GROUP, REACH)],
-            halo_send.at[1],
-            halo_recv.at[1],
-            plane(outer - 1),
-        ),
-    ]
+    coef_copies[0].wait_recv()
+    halo_copies = []
+    for side in (half, 1 - half):
+        if len(halo_copies) == 1:
+            coef_copies[1].wait_recv()
+            coef_copies[2].wait_recv()
+        halo_copies.append(
+            remote(
+                window.at[pl.ds(REACH + side * (GROUP - REACH), REACH)],
+                window.at[pl.ds((1 - side) * (REACH + GROUP), REACH)],
+                halo_send.at[side],
+                halo_recv.at[side],
+                plane(side + (1 - side) * (outer - 1)),
+            )
+        )
     pair_copies[0].wait_recv()
     pair_copies.append(
         remote(
@@ -215,14 +216,47 @@
     part[...] = density.astype(BF16).reshape(outer, share, pairs)
     part_copies = [
         remote(
-            part.at[(z + d) % outer],
-            part_in.at[d - 1],
-            part_send.at[d - 1],
-            part_recv.at[d - 1],
+            part.at[(z + d) % outer, pl.ds(c * sub, sub)],
+            part_in.at[d - 1, pl.ds(c * sub, sub)],
+            part_send.at[c, d - 1],
+            part_recv.at[c, d - 1],
             plane(d),
         )
-        for d in range(1, outer)
+        for c in range(PIECES)
+        for d in far_first
     ]
+
+    near_copies[0].wait_recv()
+    near_copies.append(
+        remote(
+            near.at[across], near.at[across], near_send.at[2], near_recv.at[2], core_mate
+        )
+    )
+    own_rows.wait()
+    pair_alpha[...] = jnp.transpose(pair_tile[...].astype(F32))
+    own_coupling.wait()
+
+    exc_copies = []
+    for c in range(PIECES):
+        piece = slice(c * sub, (c + 1) * sub)
+        for copy in part_copies[c * (outer - 1) : (c + 1) * (outer - 1)]:
+            copy.wait_recv()
+        total = part[z, piece].astype(F32)
+        for d in range(1, outer):
+            total = total + part_in[d - 1, piece].astype(F32)
+        raised = jnp.dot(total.astype(BF16), coupling[...], preferred_element_type=F32)
+        at = pl.ds(pl.multiple_of(first % lanes + c * sub, sub), sub)
+        excited[z, piece] = (raised * pair_alpha[at, :]).astype(BF16)
+        exc_copies += [
+            remote(
+                excited.at[z, pl.ds(c * sub, sub)],
+                excited.at[z, pl.ds(c * sub, sub)],
+                exc_send.at[c, d - 1],
+                exc_recv.at[c, d - 1],
+                plane(d),
+            )
+            for d in far_first
+        ]
 
     for copy in alpha_copies:
         copy.wait_recv()
@@ -246,32 +280,6 @@
 
     lax.fori_loop(0, GROUP, alpha_step, 0)
 
-    near_copies[0].wait_recv()
-    near_copies.append(
-        remote(
-            near.at[across], near.at[across], near_send.at[2], near_recv.at[2], core_mate
-        )
-    )
-    own_rows.wait()
-    pair_alpha[...] = jnp.transpose(pair_tile[...].astype(F32))
-    own_coupling.wait()
-
-    for copy in part_copies:
-        copy.wait_recv()
-    total = part[z].astype(F32)
-    for d in range(1, outer):
-        total = total + part_in[d - 1].astype(F32)
-    raised = jnp.dot(total.astype(BF16), coupling[...], preferred_element_type=F32)
-    excited[z] = (raised * pair_alpha[pl.ds(pl.multiple_of(first % lanes, share), share), :]).astype(
-        BF16
-    )
-    exc_copies = [
-        remote(
-            excited.at[z], excited.at[z], exc_send.at[d - 1], exc_recv.at[d - 1], plane(d)
-        )
-        for d in range(1, outer)
-    ]
-
     for copy in near_copies[1:]:
         copy.wait_recv()
     for copy in halo_copies:
@@ -283,38 +291,41 @@
         )
 
     back_copies = []
-    for e in range(outer):
-        if e > 0:
-            exc_copies[e - 1].wait_recv()
-        y = (z + outer - e) % outer
-        mixed = jnp.dot(excited[y], plane_pairs, preferred_element_type=F32)
-        mixed = mixed + both[pl.ds(pl.multiple_of(y * share, share), share), :]
-        for i in range(GROUP):
-            back[i, y] = mixed[:, i * width : (i + 1) * width].astype(BF16)
-        for d in range(1, GROUP):
-            back_copies.append(
-                (
-                    d,
-                    y,
-                    remote(
-                        back.at[(g + d) % GROUP, y],
-                        back_in.at[d - 1, y],
-                        back_send.at[e, d],
-                        back_recv.at[e, d],
-                        mate(d),
-                    ),
+    for c in range(PIECES):
+        piece = slice(c * sub, (c + 1) * sub)
+        for e in sorted(range(outer), key=lambda d: min(d, outer - d)):
+            if e > 0:
+                exc_copies[c * (outer - 1) + far_first.index(e)].wait_recv()
+            y = (z + outer - e) % outer
+            mixed = jnp.dot(excited[y, piece], plane_pairs, preferred_element_type=F32)
+            mixed = mixed + both[pl.ds(pl.multiple_of(y * share + c * sub, sub), sub), :]
+            for i in range(GROUP):
+                back[i, y, piece] = mixed[:, i * width : (i + 1) * width].astype(BF16)
+            for i, h in enumerate((across, opposite, beside)):
+                back_copies.append(
+                    (
+                        h,
+                        y,
+                        c,
+                        i,
+                        remote(
+                            back.at[h, y, pl.ds(c * sub, sub)],
+                            back_in.at[i, y, pl.ds(c * sub, sub)],
+                            back_send.at[c * outer + e, i],
+                            back_recv.at[c * outer + e, i],
+                            (a, z * GROUP + h),
+                        ),
+                    )
                 )
-            )
-        at = pl.ds(pl.multiple_of(g * strip + y * share, share), share)
-        out[at, :] = out[at, :] + back[g, y].astype(F32)
-    for d, y, copy in back_copies:
+            at = pl.ds(pl.multiple_of(g * strip + y * share + c * sub, sub), sub)
+            out[at, :] = out[at, :] + back[g, y, piece].astype(F32)
+    for h, y, c, i, copy in back_copies:
         copy.wait_recv()
-        h = (g + GROUP - d) % GROUP
-        at = pl.ds(pl.multiple_of(h * strip + y * share, share), share)
-        out[at, :] = out[at, :] + back_in[d - 1, y].astype(F32)
+        at = pl.ds(pl.multiple_of(h * strip + y * share + c * sub, sub), sub)
+        out[at, :] = out[at, :] + back_in[i, y, c * sub : (c + 1) * sub].astype(F32)
 
     everything = coef_copies + pair_copies + alpha_copies + near_copies + halo_copies
-    everything += part_copies + exc_copies + [copy for _, _, copy in back_copies]
+    everything += part_copies + exc_copies + [entry[-1] for entry in back_copies]
     for copy in everything:
         copy.wait_send()
 
@@ -374,12 +385,12 @@
             dma((GROUP,)),
             dma((GROUP,)),
             dma((GROUP,)),
-            dma((outer, GROUP)),
-            dma((outer, GROUP)),
-            dma((outer - 1,)),
-            dma((outer - 1,)),
-            dma((outer - 1,)),
-            dma((outer - 1,)),
+            dma((PIECES * outer, GROUP)),
+            dma((PIECES * outer, GROUP)),
+            dma((PIECES, outer - 1)),
+            dma((PIECES, outer - 1)),
+            dma((PIECES, outer - 1)),
+            dma((PIECES, outer - 1)),
             dma((2,)),
             dma((2,)),
             dma((2,)),

time: 37.1 us -> 35.3 us (0.951)
  Pallas kernels: 36 us -> 34.2 us
    pallas_call x1, Pallas kernels: 36 us -> 34.2 us  [local(): pl.pallas_call(functools.partial(kernel, n_alpha, n_beta), out_shape=pltp...]
where the time goes in v3:
time: 35.3 us; the launch traced here: 35.1 us
  Pallas kernels  34.2 us (97%)
  other arithmetic  0.87 us (2%)
    pallas_call x1, Pallas kernels, local(): pl.pallas_call(functools.partial(kernel, n_alpha, n_beta), out_shape=pltp...  34.2 us
    div x1, other arithmetic, local(): return summed / denominators  0.87 us

profile of v3, /device:TPU:0, one launch (start us, length us, event | category | flops | bytes accessed | tf_op | source)
XLA Modules:
  0.0 35.1 jit_solution(9225450935554226317)
XLA Ops:
  0.0 0.0 copy-start
  0.0 34.2 %shard_map.91 = f32[1024,128]{1,0:T(8,128)S(1)} custom-call(s32[1,4]{1,0:T(1,128)} %beta_cols.1, s32[1,4]{1,0:T(1,128)} %alpha_cols.1, bf16[1024,128]{1,0:T(8,128)(2,1)} %coef_in.1, bf16[128,512]{1,0:T(8,128)(2,1)} %ops_in.1, bf16[1024,4096]{1,0:T(8,128)(2,1)} %alpha_in.1, bf16[576,1024]{1,0:T(8,128)(2,1)} %bitcast.2, bf16[576,128]{1,0:T(8,128)(2,1)} %bitcast.3, ...), custom_call_target="tpu_custom_call" | custom-call | tf_op jit(solution)/shard_map/pallas_call | solution.py:359
  34.2 0.0 copy-done
  34.2 0.9 %div.3 = f32[1024,128]{1,0:T(8,128)} divide(f32[1024,128]{1,0:T(8,128)S(1)} %shard_map.91, f32[1024,128]{1,0:T(8,128)S(1)} %copy-done) | non-fusion elementwise | flops 131072 | bytes 1572864 | tf_op jit(solution)/shard_map/div | solution.py:401
Async XLA Ops:
  0.0 34.2 %copy-start = (f32[1024,128]{1,0:T(8,128)S(1)}, f32[1024,128]{1,0:T(8,128)}, u32[]{:S(2)}) copy-start(f32[1024,128]{1,0:T(8,128)} %param.17) | copy-start | bytes 1572868
